TPU v7x, 64 devices: a 2x2x8 block of a 4x4x8 slice. The times are simulated.
64 devices in a mesh: dp: 4 (over x, y), vp: 16 (over z, core).
Axes of the slice: x: 2, y: 2, z: 8, core: 2. Of those that a mesh axis runs over, the one named last changes fastest.
The devices are a block of a 4x4x8 slice.
Arguments:
- hidden: bfloat16 [4096, 4096], P('dp'), parts along dimension 0
- w_head: bfloat16 [4096, 32768], P(None, 'vp')
- inv_temp: float32 [4096], P('dp'), parts along dimension 0
- target_ids: int32 [4096], P('dp'), parts along dimension 0
Outputs:
- output 1: float32 [4096, 32768], P(('dp', 'vp')), parts along dimension 0
- output 2: float32 [4096], P('dp'), parts along dimension 0
There are 4 independent parts. A program takes and returns all parts, laid end to end along the dimension named above; an argument that names none is the same for every part.
All inputs are finite; a program needn't handle non-finite values.
Results may differ from a plain program's by a relative error of at most 0.001.
Values are sent between devices in bfloat16 or wider.
A program may use at most 768 MiB of HBM per device.

v0:
```python
import jax
import jax.numpy as jnp
from jax import lax
from jax.sharding import PartitionSpec as P, NamedSharding


def solution(mesh):
    group_size = mesh.shape["vp"]

    def local_step(hidden, w_local, inv_temp, target_ids):
        group_index = lax.axis_index("vp")
        local_vocab = w_local.shape[1]
        logits = jnp.dot(hidden, w_local, preferred_element_type=jnp.float32)
        scaled = logits * inv_temp[:, None]
        local_max = jnp.max(scaled, axis=1)
        exp_vals = jnp.exp(scaled - local_max[:, None])
        local_sum = jnp.sum(exp_vals, axis=1)
        shard_stats = lax.all_gather(jnp.stack([local_max, local_sum]), "vp")
        global_max = jnp.max(shard_stats[:, 0], axis=0)
        global_sum = jnp.sum(shard_stats[:, 1] * jnp.exp(shard_stats[:, 0] - global_max[None, :]), axis=0)
        row_scale = jnp.exp(local_max - global_max) / global_sum
        local_cdf = jnp.cumsum(exp_vals * row_scale[:, None], axis=1)
        totals = lax.all_gather(local_cdf[:, -1], "vp")
        earlier = (jnp.arange(group_size) < group_index)[:, None]
        offset = jnp.sum(jnp.where(earlier, totals, 0.0), axis=0)
        cdf_cols = local_cdf + offset[:, None]
        local_ids = target_ids - group_index * local_vocab
        in_shard = (local_ids >= 0) & (local_ids < local_vocab)
        picked = jnp.take_along_axis(cdf_cols, jnp.clip(local_ids, 0, local_vocab - 1)[:, None], axis=1)[:, 0]
        cdf_at_target = lax.psum(jnp.where(in_shard, picked, 0.0), "vp")
        cdf_rows = lax.all_to_all(cdf_cols, "vp", 0, 1, tiled=True)
        return cdf_rows, cdf_at_target

    return jax.shard_map(
        local_step,
        mesh=mesh,
        in_specs=(P("dp", None), P(None, "vp"), P("dp"), P("dp")),
        out_specs=(P(("dp", "vp"), None), P("dp")),
        check_vma=False,
    )
```

profile of v0, /device:TPU:21, one launch (start us, length us, event | category | flops | bytes accessed | tf_op | source)
XLA Modules:
  0.0 350.1 jit_solution(17354391285130864456)
XLA Ops:
  0.6 0.0 copy-start.1
  0.6 23.9 %multiply_reduce_fusion = (f32[1024]{0:T(1024)S(1)}, f32[1024,2048]{1,0:T(8,128)S(1)}) fusion(f32[1024]{0:T(1024)} %param.6, bf16[1024,4096]{1,0:T(8,128)(2,1)} %param.4, bf16[4096,2048]{1,0:T(8,128)(2,1)} %param.5), kind=kOutput, calls=%fused_computation.3 | convolution fusion | flops 17184063488 | bytes 33562624 | tf_op jit(solution)/shard_map/dot_general | solution.py:13
  24.5 0.0 copy-done.1
  24.5 2.0 fusion
  26.6 23.3 %all-gather.2 = f32[16,2,1024]{2,1,0:T(2,128)S(1)} all-gather(f32[1,2,1024]{2,1,0:T(2,128)S(1)} %maximum_bitcast_fusion), channel_id=2, replica_groups=mesh['dp'=4,'vp'=16] {'vp'}, dimensions={0}, use_global_device_ids=true | all-gather | bytes 139264 | tf_op jit(solution)/shard_map/all_gather | solution.py:18
  49.8 0.1 slice_reduce_fusion
  50.0 1.7 multiply_bitcast_fusion
  51.7 5.4 %copy.25 = f32[128,8,16,128]{3,2,1,0:T(8,128)} copy(f32[128,8,16,128]{3,1,2,0:T(8,128)S(1)} %multiply_bitcast_fusion) | data formatting | bytes 16777216
  57.1 8.8 %copy.18 = f32[1024,16,128]{0,1,2:T(8,128)} copy(f32[1024,16,128]{2,1,0:T(8,128)} %bitcast.36) | data formatting | bytes 16777216 | tf_op jit(solution)/shard_map/reshape.2
  65.9 7.4 %fusion.7 = f32[1024,16,128]{0,1,2:T(8,128)} fusion(f32[1024,16,128]{0,1,2:T(8,128)} %copy.18), kind=kOutput, calls=%fused_computation.27 | output fusion | flops 266338304 | bytes 16777216 | tf_op jit(solution)/shard_map/reduce-window
  73.3 0.8 slice_bitcast_fusion
  74.1 0.1 reduce-window.9
  74.2 4.4 %broadcast_add_fusion.2 = f32[1024,16,128]{0,1,2:T(8,128)S(1)} fusion(f32[1024,16,128]{0,1,2:T(8,128)} %fusion.7, f32[1024,16]{0,1:T(8,128)S(1)} %slice.26), kind=kLoop, calls=%fused_computation.7 | loop fusion | flops 2097152 | bytes 16842752 | tf_op jit(solution)/shard_map/reduce_window_sum
  78.6 0.0 copy-start
  78.6 3.4 copy-done
  82.0 8.1 %copy.20 = f32[1024,16,128]{0,2,1:T(8,128)} copy(f32[1024,16,128]{0,1,2:T(8,128)S(1)} %broadcast_add_fusion.2) | data formatting | bytes 16777216 | tf_op jit(solution)/shard_map/reduce_window_sum
  90.1 9.2 %copy.19 = f32[1024,16,128]{2,1,0:T(8,128)} copy(f32[1024,16,128]{0,1,2:T(8,128)} %copy-done) | data formatting | bytes 16777216 | tf_op jit(solution)/shard_map/reduce_window_sum
  99.3 0.8 slice.27
  100.1 14.9 %all-gather.1 = f32[16384,1]{0,1:T(1,128)S(1)} all-gather(f32[1024,1]{0,1:T(1,128)S(1)} %slice.27), channel_id=3, replica_groups=mesh['dp'=4,'vp'=16] {'vp'}, dimensions={0}, use_global_device_ids=true | all-gather | bytes 69632 | tf_op jit(solution)/shard_map/all_gather | solution.py:23
  115.0 0.5 broadcast.50
  115.5 0.8 reduce.4
  116.3 9.3 %reduce_window_sum.20 = f32[16,64,2048]{2,1,0:T(8,128)} reshape(f32[1024,16,128]{2,1,0:T(8,128)} %copy.19) | data formatting | bytes 16777216 | tf_op jit(solution)/shard_map/reduce_window_sum
  125.6 0.1 select_reduce_fusion
  125.7 0.1 add.24
  125.7 7.4 %broadcast_add_fusion.1 = f32[16,64,2048]{2,1,0:T(8,128)} fusion(f32[16,64,2048]{2,1,0:T(8,128)} %reduce_window_sum.20, f32[16,64]{1,0:T(8,128)S(1)} %add.24), kind=kLoop, calls=%fused_computation.6 | loop fusion | flops 2097152 | bytes 16781312 | tf_op jit(solution)/shard_map/add | solution.py:26
  133.1 0.0 copy-start.2
  133.1 5.1 %all-to-all-start = ((f32[16,64,2048]{2,1,0:T(8,128)}), f32[16,64,2048]{2,1,0:T(8,128)}, u32[]{:S(2)}, u32[]{:S(2)}) async-start(f32[16,64,2048]{2,1,0:T(8,128)} %broadcast_add_fusion.1), calls=%async_computation | async-start | bytes 16777216 | tf_op jit(solution)/shard_map/all_to_all | solution.py:31
  138.2 0.0 copy-done.2
  138.3 8.5 %broadcast_add_fusion = f32[1024,2048]{0,1:T(8,128)} fusion(f32[1024]{0:T(1024)S(1)} %select_reduce_fusion, f32[1024,16,128]{0,2,1:T(8,128)} %copy.20), kind=kLoop, calls=%fused_computation.5 | loop fusion | flops 2097152 | bytes 16781312 | tf_op jit(solution)/shard_map/add | solution.py:26
  146.8 42.5 %gather_fusion = f32[1024]{0:T(1024)S(1)} fusion(f32[1024,2048]{0,1:T(8,128)} %broadcast_add_fusion, s32[1024]{0:T(1024)S(1)} %bitcast.34), kind=kCustom, calls=%fused_computation | custom fusion | bytes 16384 | tf_op jit(solution)/shard_map/jit(take_along_axis)/gather | solution.py:29
  189.4 152.8 %psum.7 = f32[1024]{0:T(1024)} all-reduce(f32[1024]{0:T(1024)S(1)} %select_select_fusion), channel_id=1, replica_groups=mesh['dp'=4,'vp'=16] {'vp'}, use_global_device_ids=true, to_apply=%region_7.8 | all-reduce | flops 1024 | bytes 8192 | tf_op jit(solution)/shard_map/psum | solution.py:30
  342.2 0.0 all-to-all-done
  342.2 7.9 %copy.24 = f32[16,8,8,2048]{3,2,0,1:T(8,128)} copy(f32[16,8,8,2048]{3,2,1,0:T(8,128)} %bitcast.11) | data formatting | bytes 16777216 | tf_op jit(solution)/shard_map/all_to_all | solution.py:31
  (11 shorter events, 0.1 us)
Async XLA Ops:
  0.6 23.9 %copy-start.1 = (f32[1024]{0:T(1024)S(1)}, f32[1024]{0:T(1024)}, u32[]{:S(2)}) copy-start(f32[1024]{0:T(1024)} %param.6) | copy-start | bytes 12292
  78.6 3.4 copy-start
  133.1 5.1 %copy-start.2 = (s32[1024]{0:T(1024)S(1)}, s32[1024]{0:T(1024)}, u32[]{:S(2)}) copy-start(s32[1024]{0:T(1024)} %param.7) | copy-start | bytes 12292
  133.1 209.1 %all-to-all-start = ((f32[16,64,2048]{2,1,0:T(8,128)}), f32[16,64,2048]{2,1,0:T(8,128)}, u32[]{:S(2)}, u32[]{:S(2)}) async-start(f32[16,64,2048]{2,1,0:T(8,128)} %broadcast_add_fusion.1), calls=%async_computation | async-start | bytes 16777216 | tf_op jit(solution)/shard_map/all_to_all | solution.py:31
where the time goes:
time: 354 us; the launch traced here: 350 us
  blocking collectives  191 us (54%)
  local copies, waits for them, and re-layouts  96.8 us (27%)
  other arithmetic  32.6 us (9%)
  matrix products  23.9 us (7%)
  starting transfers between devices  5.06 us (1%)
    psum x1, blocking collectives, local_step(): cdf_at_target = lax.psum(jnp.where(in_shard, picked, 0.0), 'vp')  153 us
    gather x1, local copies, waits for them, and re-layouts, local_step(): jnp.take_along_axis(cdf_cols, jnp.clip(local_ids, 0, local_vocab - 1)[:,...  42.5 us
    another operation x6, local copies, waits for them, and re-layouts  36.2 us
    dot_general x1, matrix products, local_step(): logits = jnp.dot(hidden, w_local, preferred_element_type=jnp.float32)  23.9 us
    all_gather x1, blocking collectives, local_step(): shard_stats = lax.all_gather(jnp.stack([local_max, local_sum]), 'vp')  23.3 us
    add x2, other arithmetic, local_step(): cdf_cols = local_cdf + offset[:, None]  15.9 us
    all_gather x1, blocking collectives, local_step(): totals = lax.all_gather(local_cdf[:, -1], 'vp')  14.9 us
    another operation x3, other arithmetic  11.8 us
  transfers between devices with their start and end apart: 1, of which 0 were waited for; matrix products, arithmetic and copies ran while one was open for 15% of the time, Pallas kernels for 0%

commit v1 on v0

v1 whole, which is shorter than its diff:
```python
import functools
import jax
import jax.numpy as jnp
from jax import lax
from jax.experimental import pallas as pl
from jax.experimental.pallas import tpu as pltpu
from jax.sharding import PartitionSpec as P

MESH = pl.DeviceIdType.MESH
F32 = jnp.float32
BF16 = jnp.bfloat16
CHUNKS = 4
LANES = 128


def exchange_kernel(
    size, it_ref, tgt_ref, hid_ref, w_ref,
    recv_ref, so_ref, out_t_ref,
    w_v, hid_v, tri_v, send_v, stat_send, stat_recv,
    w_sem, h_sem, data_send, data_recv, stat_ssem, stat_rsem, t_ssem, t_rsem,
):
    me = lax.axis_index("vp")
    chips = size // 2
    z, c = me // 2, me % 2
    rows = hid_ref.shape[0] // chips
    half = rows // 2
    depth = hid_ref.shape[1]
    local_vocab = w_ref.shape[1]
    width = local_vocab // CHUNKS
    block = tri_v.shape[0]

    def chip_at(i):
        dist = chips // 2 - (i + 1) // 2
        sign = 2 * (i % 2) - 1
        return (z + sign * dist + 2 * chips) % chips

    barrier = pltpu.get_barrier_semaphore()
    for k in range(1, size):
        pl.semaphore_signal(barrier, inc=1, device_id={"vp": (me + k) % size}, device_id_type=MESH)

    parts = 4
    piece = depth // parts

    def w_copy(j, p):
        return pltpu.make_async_copy(
            w_ref.at[pl.ds(p * piece, piece), pl.ds(pl.multiple_of(j * width, width), width)],
            w_v.at[j, pl.ds(p * piece, piece)],
            w_sem.at[j, p],
        )

    def h_copy(i):
        start = pl.multiple_of(chip_at(i) * rows, rows)
        return pltpu.make_async_copy(hid_ref.at[pl.ds(start, rows)], hid_v.at[i], h_sem.at[i])

    h_copy(0).start()
    for p in range(parts):
        w_copy(0, p).start()
    r_iota = lax.broadcasted_iota(jnp.int32, (block, block), 0)
    c_iota = lax.broadcasted_iota(jnp.int32, (block, block), 1)
    tri_v[...] = jnp.where(r_iota <= c_iota, 1.0, 0.0).astype(BF16)
    h_copy(0).wait()
    for p in range(parts):
        w_copy(0, p).wait()
    for j in range(1, CHUNKS):
        for p in range(parts):
            w_copy(j, p).start()
    for i in range(1, chips):
        h_copy(i).start()

    lane = lax.broadcasted_iota(jnp.int32, (rows, LANES), 1)

    def to_column(row):
        return jnp.transpose(jnp.broadcast_to(row, (LANES, LANES)))[:, :1]

    def row_params(i):
        chip = chip_at(i)
        temp = to_column(it_ref[pl.ds(chip, 1)])
        target = to_column((tgt_ref[pl.ds(chip, 1)] - me * local_vocab).astype(F32))
        return temp, target

    def chunk(i, j, temp, target, state):
        top, carry, pick, stats = state
        logits = jnp.dot(hid_v[i], w_v[j], preferred_element_type=F32) * temp
        new_top = jnp.maximum(top, jnp.max(logits, axis=1, keepdims=True))
        drop = jnp.exp(top - new_top)
        carry = carry * drop
        pick = pick * drop
        e = jnp.exp(logits - new_top)
        first = e.astype(BF16)
        rest = e - first.astype(F32)
        second = rest.astype(BF16)
        third = (rest - second.astype(F32)).astype(BF16)
        col = lax.broadcasted_iota(jnp.int32, (rows, block), 1).astype(F32)
        base = (j * width).astype(F32) if not isinstance(j, int) else float(j * width)
        for t in range(width // block):
            cut = slice(t * block, (t + 1) * block)
            terms = jnp.concatenate([first[:, cut], second[:, cut], third[:, cut]], axis=0)
            sums = jnp.dot(terms, tri_v[...], preferred_element_type=F32)
            run = (sums[:rows] + (sums[rows : 2 * rows] + sums[2 * rows :])) + carry
            send_v[i, j, :, pl.ds(t * block, block)] = run
            hit = (col + (base + float(t * block))) == target
            pick = pick + jnp.sum(jnp.where(hit, run, 0.0), axis=1, keepdims=True)
            carry = run[:, block - 1 :]
        stats = jnp.where(lane == j, new_top, stats)
        return new_top, carry, pick, stats

    def send_data(i, j):
        for core in range(2):
            pltpu.make_async_remote_copy(
                src_ref=send_v.at[i, j, pl.ds(core * half, half)],
                dst_ref=recv_ref.at[me * CHUNKS + j],
                send_sem=data_send.at[i],
                recv_sem=data_recv.at[me],
                device_id={"vp": chip_at(i) * 2 + core},
                device_id_type=MESH,
            ).start()

    def start_state():
        column = jnp.zeros((rows, 1), F32)
        return column - jnp.inf, column, column, jnp.zeros((rows, LANES), F32)

    def finish(i, state):
        _, carry, pick, stats = state
        stats = jnp.where(lane == CHUNKS, carry, stats)
        stats = jnp.where(lane == CHUNKS + 1, pick, stats)
        stat_send[i] = jnp.transpose(stats)[:8]

    temp0, target0 = row_params(0)
    state0 = chunk(0, 0, temp0, target0, start_state())
    pl.semaphore_wait(barrier, size - 1)
    send_data(0, 0)

    def first_step(j, state):
        for p in range(parts):
            w_copy(j, p).wait()
        state = chunk(0, j, temp0, target0, state)
        send_data(0, j)
        return state

    finish(0, lax.fori_loop(1, CHUNKS, first_step, state0))

    early = 3

    def step(i, carry_):
        h_copy(i).wait()
        temp, target = row_params(i)

        def inner(j, state):
            state = chunk(i, j, temp, target, state)

            @pl.when(i < early)
            def _():
                send_data(i, j)

            return state

        finish(i, lax.fori_loop(0, CHUNKS, inner, start_state()))
        return carry_

    lax.fori_loop(1, chips, step, 0)
    last = chips - 1

    def stat_copy(i, core):
        return pltpu.make_async_remote_copy(
            src_ref=stat_send.at[i],
            dst_ref=stat_recv.at[me],
            send_sem=stat_ssem.at[i * 2 + core],
            recv_sem=stat_rsem.at[me],
            device_id={"vp": chip_at(i) * 2 + core},
            device_id_type=MESH,
        )

    def partner_stat():
        return pltpu.make_async_remote_copy(
            src_ref=stat_send.at[last],
            dst_ref=stat_recv.at[me],
            send_sem=stat_ssem.at[last * 2],
            recv_sem=stat_rsem.at[me],
            device_id={"vp": z * 2 + (1 - c)},
            device_id_type=MESH,
        )

    for i in range(last):
        for core in range(2):
            stat_copy(i, core).start()
    partner_stat().start()
    stat_recv[me] = stat_send[last]

    def send_step(i, carry_):
        for j in range(CHUNKS):
            send_data(i, j)
        return carry_

    lax.fori_loop(early, early + 2, send_step, 0)

    def partner_data(j):
        return pltpu.make_async_remote_copy(
            src_ref=send_v.at[last, j, pl.ds(pl.multiple_of((1 - c) * half, half), half)],
            dst_ref=recv_ref.at[me * CHUNKS + j],
            send_sem=data_send.at[last],
            recv_sem=data_recv.at[me],
            device_id={"vp": z * 2 + (1 - c)},
            device_id_type=MESH,
        )

    for j in range(CHUNKS):
        partner_data(j).start()
    for j in range(CHUNKS):
        recv_ref[me * CHUNKS + j] = send_v[last, j, pl.ds(pl.multiple_of(c * half, half), half)]

    def wait_stat(k, carry_):
        src = (me + k) % size
        pltpu.make_async_remote_copy(
            src_ref=stat_send.at[0], dst_ref=stat_recv.at[src],
            send_sem=stat_ssem.at[0], recv_sem=stat_rsem.at[src],
            device_id={"vp": src}, device_id_type=MESH,
        ).wait_recv()
        return carry_

    lax.fori_loop(1, size, wait_stat, 0)
    tops = [stat_recv[s, CHUNKS - 1 : CHUNKS] for s in range(size)]
    global_top = functools.reduce(jnp.maximum, tops)
    weights = [jnp.exp(t - global_top) for t in tops]
    masses = [stat_recv[s, CHUNKS : CHUNKS + 1] * weights[s] for s in range(size)]
    inverse = 1.0 / functools.reduce(lambda a, b: a + b, masses)
    offsets = [jnp.zeros((1, rows), F32)]
    for s in range(size - 1):
        offsets.append(offsets[-1] + masses[s])
    ids = tgt_ref[pl.ds(z, 1)]
    value = jnp.zeros((1, rows), F32)
    for s in range(size):
        inside = (ids >= s * local_vocab) & (ids < (s + 1) * local_vocab)
        here = stat_recv[s, CHUNKS + 1 : CHUNKS + 2] * weights[s] + offsets[s]
        value = value + jnp.where(inside, here, 0.0)
    out_t_ref[pl.ds(z, 1)] = value * inverse

    def t_copy(k):
        return pltpu.make_async_remote_copy(
            src_ref=out_t_ref.at[pl.ds(z, 1)],
            dst_ref=out_t_ref.at[pl.ds(z, 1)],
            send_sem=t_ssem.at[k],
            recv_sem=t_rsem.at[z],
            device_id={"vp": ((z + k) % chips) * 2 + c},
            device_id_type=MESH,
        )

    for k in range(1, chips):
        t_copy(k).start()

    lax.fori_loop(early + 2, last, send_step, 0)

    scales = [jnp.exp(stat_recv[s, :CHUNKS] - global_top) * inverse for s in range(size)]
    table = jnp.concatenate(scales + [o * inverse for o in offsets], axis=0)
    pad = LANES - table.shape[0]
    if pad:
        table = jnp.concatenate([table, jnp.zeros((pad, rows), F32)], axis=0)
    turned = jnp.transpose(table)
    so_ref[...] = jnp.where(c == 0, turned[:half], turned[half:])

    def wait_sends(i, carry_):
        pltpu.make_async_remote_copy(
            src_ref=send_v.at[i], dst_ref=send_v.at[i], send_sem=data_send.at[i], recv_sem=data_recv.at[0],
            device_id={"vp": chip_at(i) * 2}, device_id_type=MESH,
        ).wait_send()
        for core in range(2):
            stat_copy(i, core).wait_send()
        return carry_

    lax.fori_loop(0, last, wait_sends, 0)
    partner_stat().wait_send()
    for k in range(1, chips):
        t_copy(k).wait_send()
    mine = pl.ds(pl.multiple_of((1 - c) * half, half), half)
    pltpu.make_async_remote_copy(
        src_ref=send_v.at[last, :, mine], dst_ref=send_v.at[last, :, mine],
        send_sem=data_send.at[last], recv_sem=data_recv.at[0],
        device_id={"vp": z * 2 + (1 - c)}, device_id_type=MESH,
    ).wait_send()

    def wait_t(k, carry_):
        src = (z + k) % chips
        pltpu.make_async_remote_copy(
            src_ref=out_t_ref.at[pl.ds(src, 1)], dst_ref=out_t_ref.at[pl.ds(src, 1)],
            send_sem=t_ssem.at[0], recv_sem=t_rsem.at[src],
            device_id={"vp": src * 2 + c}, device_id_type=MESH,
        ).wait_recv()
        return carry_

    lax.fori_loop(1, chips, wait_t, 0)

    def wait_data(k, carry_):
        src = (me + k) % size
        there = recv_ref.at[pl.ds(src * CHUNKS, CHUNKS)]
        pltpu.make_async_remote_copy(
            src_ref=there, dst_ref=there, send_sem=data_send.at[0], recv_sem=data_recv.at[src],
            device_id={"vp": src}, device_id_type=MESH,
        ).wait_recv()
        return carry_

    lax.fori_loop(1, size, wait_data, 0)


def table_kernel(size, recv_ref, so_ref, t_ref, table_ref, out_t_ref, stage, sems, t_sem):
    width = recv_ref.shape[2]
    t_out = pltpu.make_async_copy(t_ref, out_t_ref, t_sem)
    t_out.start()
    copies = []
    for s in range(size):
        offset = so_ref[:, size * CHUNKS + s : size * CHUNKS + s + 1]
        for j in range(CHUNKS):
            k = s * CHUNKS + j
            stage[s, :, j * width : (j + 1) * width] = recv_ref[k] * so_ref[:, k : k + 1] + offset
        shard = CHUNKS * width
        copy = pltpu.make_async_copy(stage.at[s], table_ref.at[:, pl.ds(s * shard, shard)], sems.at[s])
        copy.start()
        copies.append(copy)
    t_out.wait()
    for copy in copies:
        copy.wait()


def solution(mesh):
    size = mesh.shape["vp"]
    chips = size // 2

    def local_step(hidden, w_local, inv_temp, target_ids):
        batch, depth = hidden.shape
        local_vocab = w_local.shape[1]
        width = local_vocab // CHUNKS
        rows = batch // chips
        half = rows // 2
        block = min(256, width)
        vmem = pl.BlockSpec(memory_space=pltpu.VMEM)
        hbm = pl.BlockSpec(memory_space=pl.ANY)
        recv, so, t_all = pl.pallas_call(
            functools.partial(exchange_kernel, size),
            out_shape=(
                pltpu.VMEM((size * CHUNKS, half, width), F32),
                pltpu.VMEM((half, LANES), F32),
                pltpu.VMEM((chips, rows), F32),
            ),
            in_specs=[vmem, vmem, hbm, hbm],
            out_specs=(vmem, vmem, vmem),
            scratch_shapes=[
                pltpu.VMEM((CHUNKS, depth, width), BF16),
                pltpu.VMEM((chips, rows, depth), BF16),
                pltpu.VMEM((block, block), BF16),
                pltpu.VMEM((chips, CHUNKS, rows, width), F32),
                pltpu.VMEM((chips, 8, rows), F32),
                pltpu.VMEM((size, 8, rows), F32),
                pltpu.SemaphoreType.DMA((CHUNKS, 4)),
                pltpu.SemaphoreType.DMA((chips,)),
                pltpu.SemaphoreType.DMA((chips,)),
                pltpu.SemaphoreType.DMA((size,)),
                pltpu.SemaphoreType.DMA((size,)),
                pltpu.SemaphoreType.DMA((size,)),
                pltpu.SemaphoreType.DMA((chips,)),
                pltpu.SemaphoreType.DMA((chips,)),
            ],
            compiler_params=pltpu.CompilerParams(
                collective_id=0, has_side_effects=True, vmem_limit_bytes=46 * 1024 * 1024
            ),
            name="exchange",
        )(inv_temp.reshape(chips, rows), target_ids.reshape(chips, rows), hidden, w_local)
        recv, so, t_all = [pltpu.with_memory_space_constraint(x, pltpu.VMEM) for x in (recv, so, t_all)]
        table, cdf_at_target = pl.pallas_call(
            functools.partial(table_kernel, size),
            out_shape=(
                jax.ShapeDtypeStruct((half, size * local_vocab), F32),
                jax.ShapeDtypeStruct((chips, rows), F32),
            ),
            in_specs=[vmem, vmem, vmem],
            out_specs=(hbm, hbm),
            scratch_shapes=[
                pltpu.VMEM((size, half, local_vocab), F32),
                pltpu.SemaphoreType.DMA((size,)),
                pltpu.SemaphoreType.DMA,
            ],
            compiler_params=pltpu.CompilerParams(vmem_limit_bytes=24 * 1024 * 1024),
            name="table",
        )(recv, so, t_all)
        return table, cdf_at_target.reshape(batch)

    return jax.shard_map(
        local_step,
        mesh=mesh,
        in_specs=(P("dp", None), P(None, "vp"), P("dp"), P("dp")),
        out_specs=(P(("dp", "vp"), None), P("dp")),
        check_vma=False,
    )
```

time: 354 us -> 201 us (0.57); the launches traced: 350 us -> 201 us
  Pallas kernels: 0 us -> 200 us
  blocking collectives: 191 us -> 0 us
  local copies, waits for them, and re-layouts: 96.8 us -> 0 us
  other arithmetic: 32.6 us -> 0 us
  matrix products: 23.9 us -> 0 us
  starting transfers between devices: 5.06 us -> 0 us
    pallas_call x0 -> x2, Pallas kernels: none -> 200 us  [the longest x1 197 us: local_step(): pl.pallas_call(functools.partial(exchange_kernel, size), out_shape=(pltpu...]
    psum x1 -> x0, blocking collectives: 153 us -> none  [local_step(): cdf_at_target = lax.psum(jnp.where(in_shard, picked, 0.0), 'vp')]
    gather x1 -> x0, local copies, waits for them, and re-layouts: 42.5 us -> none  [local_step(): jnp.take_along_axis(cdf_cols, jnp.clip(local_ids, 0, local_vocab - 1)[:,...]
    all_gather x2 -> x0, blocking collectives: 38.2 us -> none  [the longest x1 23.3 us: local_step(): shard_stats = lax.all_gather(jnp.stack([local_max, local_sum]), 'vp')]
    another operation x6 -> x0, local copies, waits for them, and re-layouts: 36.2 us -> none
    dot_general x1 -> x0, matrix products: 23.9 us -> none  [local_step(): logits = jnp.dot(hidden, w_local, preferred_element_type=jnp.float32)]
    add x2 -> x0, other arithmetic: 15.9 us -> none  [local_step(): cdf_cols = local_cdf + offset[:, None]]
    another operation x3 -> x0, other arithmetic: 11.8 us -> none
  transfers between devices with their start and end apart: 1 -> 0, of which waited for: 0 -> 0; matrix products, arithmetic and copies ran while one was open for 15% -> 0% of each run, Pallas kernels for 0% -> 0%
where the time goes in v1:
time: 201 us
  Pallas kernels  200 us (100%)
    pallas_call x1, Pallas kernels, local_step(): pl.pallas_call(functools.partial(exchange_kernel, size), out_shape=(pltpu...  197 us

profile of v1, /device:TPU:21, one launch (start us, length us, event | category | flops | bytes accessed | tf_op | source)
XLA Modules:
  0.0 201.0 jit_solution(17564900824999657730)
XLA Ops:
  0.6 196.8 %exchange.1 = (f32[64,64,512]{2,1,0:T(8,128)S(1)}, f32[64,128]{1,0:T(8,128)S(1)}, f32[8,128]{1,0:T(8,128)S(1)}) custom-call(f32[8,128]{1,0:T(8,128)} %bitcast.3, s32[8,128]{1,0:T(8,128)} %bitcast.4, bf16[1024,4096]{1,0:T(8,128)(2,1)} %hid_ref.1, bf16[4096,2048]{1,0:T(8,128)(2,1)} %w_ref.1), custom_call_target="tpu_custom_call" | custom-call | tf_op jit(solution)/shard_map/exchange/pallas_call | solution.py:335
  197.4 3.5 %table.1 = (f32[64,32768]{1,0:T(8,128)}, f32[8,128]{1,0:T(8,128)}) custom-call(f32[64,64,512]{2,1,0:T(8,128)S(1)} %get-tuple-element.7.recv_ref, f32[64,128]{1,0:T(8,128)S(1)} %get-tuple-element.8.so_ref, f32[8,128]{1,0:T(8,128)S(1)} %get-tuple-element.9.t_ref), custom_call_target="tpu_custom_call" | custom-call | tf_op jit(solution)/shard_map/table/pallas_call | solution.py:366

commit v2 on v0

v2 whole, which is shorter than its diff:
```python
import functools
import jax
import jax.numpy as jnp
from jax import lax
from jax.experimental import pallas as pl
from jax.experimental.pallas import tpu as pltpu
from jax.sharding import PartitionSpec as P

MESH = pl.DeviceIdType.MESH
F32 = jnp.float32
BF16 = jnp.bfloat16
LANES = 128
EIGHTHS = (1, 3, 4)
CHUNKS = len(EIGHTHS)
STATS = CHUNKS + 2


def chunk_bounds(local_vocab):
    bounds, start = [], 0
    for part in EIGHTHS:
        bounds.append((start, part * local_vocab // 8))
        start += part * local_vocab // 8
    return bounds


def exchange_kernel(
    size, it_hbm, tgt_hbm, hid_ref, w_ref,
    recv_ref, so_ref, out_t_ref,
    it_ref, tgt_ref, w_v, hid_v, tri_v, send_v, stat_mine, stat_recv, t_mine, t_recv,
    row_sem, w_sem, h_sem, h0_sem, data_send, data_recv, stat_ssem, stat_rsem, pair_ssem, pair_rsem, t_ssem, t_rsem,
):
    me = lax.axis_index("vp")
    chips = size // 2
    z, c = me // 2, me % 2
    rows = hid_ref.shape[0] // chips
    half = rows // 2
    depth = hid_ref.shape[1]
    local_vocab = w_ref.shape[1]
    bounds = chunk_bounds(local_vocab)
    block = tri_v.shape[0]

    pairs = chips // 2

    def chip_at(p, side):
        steps = pairs - 1 - p
        return (z + steps) % chips if side == 0 else (z - steps + pairs * (p // (pairs - 1)) + chips) % chips

    barrier = pltpu.get_barrier_semaphore()
    parts = w_sem.shape[1]
    piece = depth // parts

    def w_copy(j, p):
        start, width = bounds[j]
        here = (pl.ds(p * piece, piece), pl.ds(start, width))
        return pltpu.make_async_copy(w_ref.at[here], w_v.at[here], w_sem.at[j, p])

    def h_copy(p, side):
        start = pl.multiple_of(chip_at(p, side) * rows, rows)
        return pltpu.make_async_copy(
            hid_ref.at[pl.ds(start, rows)], hid_v.at[p, pl.ds(side * rows, rows)], h_sem.at[p, side]
        )

    def h_first(q, side):
        start = pl.multiple_of(chip_at(0, side) * rows, rows)
        here = pl.ds(q * piece, piece)
        return pltpu.make_async_copy(
            hid_ref.at[pl.ds(start, rows), here], hid_v.at[0, pl.ds(side * rows, rows), here], h0_sem.at[q, side]
        )

    row_copies = [
        pltpu.make_async_copy(it_hbm, it_ref, row_sem.at[0]),
        pltpu.make_async_copy(tgt_hbm, tgt_ref, row_sem.at[1]),
    ]
    for q in range(parts):
        for side in range(2):
            h_first(q, side).start()
        w_copy(0, q).start()
    for copy in row_copies:
        copy.start()
    for k in range(1, size):
        pl.semaphore_signal(barrier, inc=1, device_id={"vp": (me + k) % size}, device_id_type=MESH)
    r_iota = lax.broadcasted_iota(jnp.int32, (block, block), 0)
    c_iota = lax.broadcasted_iota(jnp.int32, (block, block), 1)
    tri_v[...] = jnp.where(r_iota <= c_iota, 1.0, 0.0).astype(BF16)

    lane = lax.broadcasted_iota(jnp.int32, (2 * rows, LANES), 1)

    def to_column(row):
        return jnp.transpose(jnp.broadcast_to(row, (LANES, LANES)))[:, :1]

    def row_params(p):
        chip = [chip_at(p, side) for side in range(2)]
        temp = [to_column(it_ref[pl.ds(k, 1)]) for k in chip]
        target = [to_column((tgt_ref[pl.ds(k, 1)] - me * local_vocab).astype(F32)) for k in chip]
        return jnp.concatenate(temp, axis=0), jnp.concatenate(target, axis=0)

    def product(p, j):
        start, width = bounds[j]
        return jnp.dot(hid_v[p], w_v[:, start : start + width], preferred_element_type=F32)

    def first_product():
        width = bounds[0][1]
        total = jnp.zeros((2 * rows, width), F32)
        for q in range(parts):
            for side in range(2):
                h_first(q, side).wait()
            w_copy(0, q).wait()
            w_copy(1, q).start()
            here = slice(q * piece, (q + 1) * piece)
            total = total + jnp.dot(hid_v[0, :, here], w_v[here, :width], preferred_element_type=F32)
        return total

    def chunk(p, j, logits, temp, target, state):
        top, carry, pick, stats = state
        first_col, width = bounds[j]
        logits = logits * temp
        new_top = jnp.maximum(top, jnp.max(logits, axis=1, keepdims=True))
        drop = jnp.exp(top - new_top)
        carry = carry * drop
        pick = pick * drop
        e = jnp.exp(logits - new_top)
        first = e.astype(BF16)
        rest = e - first.astype(F32)
        second = rest.astype(BF16)
        third = (rest - second.astype(F32)).astype(BF16)
        col = lax.broadcasted_iota(jnp.int32, (2 * rows, block), 1).astype(F32)
        for t in range(width // block):
            cut = slice(t * block, (t + 1) * block)
            terms = jnp.concatenate([first[:, cut], second[:, cut], third[:, cut]], axis=0)
            sums = jnp.dot(terms, tri_v[...], preferred_element_type=F32)
            run = (sums[: 2 * rows] + (sums[2 * rows : 4 * rows] + sums[4 * rows :])) + carry
            base = first_col + t * block
            send_v[p, :, base : base + block] = run
            hit = (col + float(base)) == target
            pick = pick + jnp.sum(jnp.where(hit, run, 0.0), axis=1, keepdims=True)
            carry = run[:, block - 1 :]
        stats = jnp.where(lane == j, new_top, stats)
        return new_top, carry, pick, stats

    def send(p, side, columns):
        for core in range(2):
            pltpu.make_async_remote_copy(
                src_ref=send_v.at[p, pl.ds(side * rows + core * half, half), columns],
                dst_ref=recv_ref.at[me, :, columns],
                send_sem=data_send.at[p, side],
                recv_sem=data_recv.at[me],
                device_id={"vp": chip_at(p, side) * 2 + core},
                device_id_type=MESH,
            ).start()

    whole = pl.ds(0, local_vocab)

    def start_state():
        column = jnp.zeros((2 * rows, 1), F32)
        return column - jnp.inf, column, column, jnp.zeros((2 * rows, LANES), F32)

    def finish(p, state):
        _, carry, pick, stats = state
        stats = jnp.where(lane == CHUNKS, carry, stats)
        stats = jnp.where(lane == CHUNKS + 1, pick, stats)
        for side in range(2):
            stat_mine[c, p, side] = jnp.transpose(stats[side * rows : (side + 1) * rows])[:STATS]

    for copy in row_copies:
        copy.wait()
    temp0, target0 = row_params(0)
    state = chunk(0, 0, first_product(), temp0, target0, start_state())
    pl.semaphore_wait(barrier, size - 1)
    for side in range(2):
        send(0, side, pl.ds(*bounds[0]))
    for j in range(2, CHUNKS):
        for q in range(parts):
            w_copy(j, q).start()
    for p in range(1, pairs):
        for side in range(2):
            h_copy(p, side).start()
    for j in range(1, CHUNKS):
        for q in range(parts):
            w_copy(j, q).wait()
        state = chunk(0, j, product(0, j), temp0, target0, state)
        for side in range(2):
            send(0, side, pl.ds(*bounds[j]))
    finish(0, state)

    def step(p, carry_):
        for side in range(2):
            h_copy(p, side).wait()
        temp, target = row_params(p)
        state = start_state()
        for j in range(CHUNKS):
            state = chunk(p, j, product(p, j), temp, target, state)
        finish(p, state)
        return carry_

    lax.fori_loop(1, pairs, step, 0)
    two, one, ends = range(1, pairs)
    others = [(p, side) for p in range(pairs) for side in range(2) if (p, side) != (ends, 0)]

    partner = z * 2 + (1 - c)

    def swap(k, mine, theirs):
        there = pltpu.make_async_remote_copy(
            src_ref=mine, dst_ref=mine, send_sem=pair_ssem.at[k], recv_sem=pair_rsem.at[k],
            device_id={"vp": partner}, device_id_type=MESH,
        )
        here = pltpu.make_async_remote_copy(
            src_ref=theirs, dst_ref=theirs, send_sem=pair_ssem.at[k], recv_sem=pair_rsem.at[k],
            device_id={"vp": partner}, device_id_type=MESH,
        )
        there.start()
        there.wait_send()
        here.wait_recv()

    swap(0, stat_mine.at[c], stat_mine.at[1 - c])

    def chip_on_side(p):
        steps = pairs - 1 - p
        return (z + (1 - 2 * c) * steps + c * pairs * (p // (pairs - 1)) + chips) % chips

    def stat_copy(p):
        return pltpu.make_async_remote_copy(
            src_ref=stat_mine.at[:, p, c],
            dst_ref=stat_recv.at[c, :, p],
            send_sem=stat_ssem.at[p],
            recv_sem=stat_rsem.at[p],
            device_id={"vp": chip_on_side(p) * 2 + c},
            device_id_type=MESH,
        )

    def t_copy(p):
        return pltpu.make_async_remote_copy(
            src_ref=t_mine,
            dst_ref=t_recv.at[c, pl.ds(p, 1)],
            send_sem=t_ssem.at[p],
            recv_sem=t_rsem.at[p],
            device_id={"vp": chip_on_side(p) * 2 + c},
            device_id_type=MESH,
        )

    def slot(chip):
        steps = (z - chip + chips) % chips
        side = steps // pairs
        return side, (1 - side) * (pairs - 1 - steps % pairs) + side * ((steps + pairs - 1) % pairs)

    for p in range(ends):
        stat_copy(p).start()

    @pl.when(c == 0)
    def _():
        stat_recv[0, :, ends] = stat_mine[:, ends, 0]

    @pl.when(c == 1)
    def _():
        stat_copy(ends).start()

    for side in range(2):
        send(one, side, whole)
    send(ends, 1, whole)

    theirs = pl.ds(pl.multiple_of((1 - c) * half, half), half)
    mine = pl.ds(pl.multiple_of(c * half, half), half)
    partner_data = pltpu.make_async_remote_copy(
        src_ref=send_v.at[ends, theirs],
        dst_ref=recv_ref.at[me],
        send_sem=data_send.at[ends, 0],
        recv_sem=data_recv.at[me],
        device_id={"vp": partner},
        device_id_type=MESH,
    )
    partner_data.start()
    recv_ref[me] = send_v[ends, mine]

    for p in range(ends):
        stat_copy(p).wait_recv()

    @pl.when(c == 1)
    def _():
        stat_copy(ends).wait_recv()

    swap(1, stat_recv.at[c], stat_recv.at[1 - c])
    shards = []
    for chip in range(chips):
        side, pair = slot(chip)
        shards += [stat_recv[side, core, pair] for core in range(2)]
    tops = [x[CHUNKS - 1 : CHUNKS] for x in shards]
    global_top = functools.reduce(jnp.maximum, tops)
    weights = [jnp.exp(t - global_top) for t in tops]
    masses = [x[CHUNKS : CHUNKS + 1] * w for x, w in zip(shards, weights)]
    inverse = 1.0 / functools.reduce(lambda a, b: a + b, masses)
    offsets = [jnp.zeros((1, rows), F32)]
    for s in range(size - 1):
        offsets.append(offsets[-1] + masses[s])
    ids = tgt_ref[pl.ds(z, 1)]
    value = jnp.zeros((1, rows), F32)
    for s in range(size):
        inside = (ids >= s * local_vocab) & (ids < (s + 1) * local_vocab)
        here = shards[s][CHUNKS + 1 : CHUNKS + 2] * weights[s] + offsets[s]
        value = value + jnp.where(inside, here, 0.0)
    t_mine[...] = value * inverse
    for p in range(ends):
        t_copy(p).start()

    @pl.when(c == 0)
    def _():
        t_recv[0, ends : ends + 1] = t_mine[...]

    @pl.when(c == 1)
    def _():
        t_copy(ends).start()

    for side in range(2):
        send(two, side, whole)

    scales = [jnp.exp(x[:CHUNKS] - global_top) * inverse for x in shards]
    table = jnp.concatenate(scales + [o * inverse for o in offsets], axis=0)
    pad = LANES - table.shape[0]
    if pad:
        table = jnp.concatenate([table, jnp.zeros((pad, rows), F32)], axis=0)
    turned = jnp.transpose(table)
    so_ref[...] = jnp.where(c == 0, turned[:half], turned[half:])

    for p in range(ends):
        t_copy(p).wait_recv()

    @pl.when(c == 1)
    def _():
        t_copy(ends).wait_recv()

    swap(2, t_recv.at[c], t_recv.at[1 - c])
    for chip in range(chips):
        side, pair = slot(chip)
        out_t_ref[chip : chip + 1] = t_recv[side, pl.ds(pair, 1)]
    for p in range(ends):
        stat_copy(p).wait_send()
        t_copy(p).wait_send()

    @pl.when(c == 1)
    def _():
        stat_copy(ends).wait_send()
        t_copy(ends).wait_send()

    for p, side in others:
        gone = send_v.at[p, pl.ds(side * rows, rows)]
        pltpu.make_async_remote_copy(
            src_ref=gone, dst_ref=gone, send_sem=data_send.at[p, side], recv_sem=data_recv.at[0],
            device_id={"vp": chip_at(p, side) * 2}, device_id_type=MESH,
        ).wait_send()
    partner_data.wait_send()

    def wait_data(k, carry_):
        src = (me + k) % size
        there = recv_ref.at[src]
        pltpu.make_async_remote_copy(
            src_ref=there, dst_ref=there, send_sem=data_send.at[0, 0], recv_sem=data_recv.at[src],
            device_id={"vp": src}, device_id_type=MESH,
        ).wait_recv()
        return carry_

    lax.fori_loop(1, size, wait_data, 0)


def table_kernel(size, recv_ref, so_ref, t_ref, table_ref, out_t_ref, stage, sems, t_sem):
    shard = recv_ref.shape[2]
    t_out = pltpu.make_async_copy(t_ref, out_t_ref, t_sem)
    t_out.start()
    copies = []
    for s in range(size):
        offset = so_ref[:, size * CHUNKS + s : size * CHUNKS + s + 1]
        for j, (start, width) in enumerate(chunk_bounds(shard)):
            k = s * CHUNKS + j
            cut = slice(start, start + width)
            stage[s, :, cut] = recv_ref[s, :, cut] * so_ref[:, k : k + 1] + offset
        copy = pltpu.make_async_copy(stage.at[s], table_ref.at[:, pl.ds(s * shard, shard)], sems.at[s])
        copy.start()
        copies.append(copy)
    t_out.wait()
    for copy in copies:
        copy.wait()


def solution(mesh):
    size = mesh.shape["vp"]
    chips = size // 2
    assert chips == 8

    def local_step(hidden, w_local, inv_temp, target_ids):
        batch, depth = hidden.shape
        local_vocab = w_local.shape[1]
        rows = batch // chips
        half = rows // 2
        block = min(256, local_vocab // 8)
        vmem = pl.BlockSpec(memory_space=pltpu.VMEM)
        hbm = pl.BlockSpec(memory_space=pl.ANY)
        recv, so, t_all = pl.pallas_call(
            functools.partial(exchange_kernel, size),
            out_shape=(
                pltpu.VMEM((size, half, local_vocab), F32),
                pltpu.VMEM((half, LANES), F32),
                pltpu.VMEM((chips, rows), F32),
            ),
            in_specs=[hbm, hbm, hbm, hbm],
            out_specs=(vmem, vmem, vmem),
            scratch_shapes=[
                pltpu.VMEM((chips, rows), F32),
                pltpu.VMEM((chips, rows), jnp.int32),
                pltpu.VMEM((depth, local_vocab), BF16),
                pltpu.VMEM((chips // 2, 2 * rows, depth), BF16),
                pltpu.VMEM((block, block), BF16),
                pltpu.VMEM((chips // 2, 2 * rows, local_vocab), F32),
                pltpu.VMEM((2, chips // 2, 2, STATS, rows), F32),
                pltpu.VMEM((2, 2, chips // 2, STATS, rows), F32),
                pltpu.VMEM((1, rows), F32),
                pltpu.VMEM((2, chips // 2, rows), F32),
                pltpu.SemaphoreType.DMA((2,)),
                pltpu.SemaphoreType.DMA((CHUNKS, 4)),
                pltpu.SemaphoreType.DMA((chips // 2, 2)),
                pltpu.SemaphoreType.DMA((4, 2)),
                pltpu.SemaphoreType.DMA((chips // 2, 2)),
                pltpu.SemaphoreType.DMA((size,)),
                pltpu.SemaphoreType.DMA((chips // 2,)),
                pltpu.SemaphoreType.DMA((chips // 2,)),
                pltpu.SemaphoreType.DMA((3,)),
                pltpu.SemaphoreType.DMA((3,)),
                pltpu.SemaphoreType.DMA((chips // 2,)),
                pltpu.SemaphoreType.DMA((chips // 2,)),
            ],
            compiler_params=pltpu.CompilerParams(
                collective_id=0, has_side_effects=True, vmem_limit_bytes=46 * 1024 * 1024
            ),
            name="exchange",
        )(inv_temp.reshape(chips, rows), target_ids.reshape(chips, rows), hidden, w_local)
        recv, so, t_all = [pltpu.with_memory_space_constraint(x, pltpu.VMEM) for x in (recv, so, t_all)]
        table, cdf_at_target = pl.pallas_call(
            functools.partial(table_kernel, size),
            out_shape=(
                jax.ShapeDtypeStruct((half, size * local_vocab), F32),
                jax.ShapeDtypeStruct((chips, rows), F32),
            ),
            in_specs=[vmem, vmem, vmem],
            out_specs=(hbm, hbm),
            scratch_shapes=[
                pltpu.VMEM((size, half, local_vocab), F32),
                pltpu.SemaphoreType.DMA((size,)),
                pltpu.SemaphoreType.DMA,
            ],
            compiler_params=pltpu.CompilerParams(vmem_limit_bytes=24 * 1024 * 1024),
            name="table",
        )(recv, so, t_all)
        return table, cdf_at_target.reshape(batch)

    return jax.shard_map(
        local_step,
        mesh=mesh,
        in_specs=(P("dp", None), P(None, "vp"), P("dp"), P("dp")),
        out_specs=(P(("dp", "vp"), None), P("dp")),
        check_vma=False,
    )
```

time: 354 us -> 198 us (0.56); the launches traced: 350 us -> 198 us
  Pallas kernels: 0 us -> 197 us
  blocking collectives: 191 us -> 0 us
  local copies, waits for them, and re-layouts: 96.8 us -> 0 us
  other arithmetic: 32.6 us -> 0 us
  matrix products: 23.9 us -> 0 us
  starting transfers between devices: 5.06 us -> 0 us
    pallas_call x0 -> x2, Pallas kernels: none -> 197 us  [the longest x1 194 us: local_step(): pl.pallas_call(functools.partial(exchange_kernel, size), out_shape=(pltpu...]
    psum x1 -> x0, blocking collectives: 153 us -> none  [local_step(): cdf_at_target = lax.psum(jnp.where(in_shard, picked, 0.0), 'vp')]
    gather x1 -> x0, local copies, waits for them, and re-layouts: 42.5 us -> none  [local_step(): jnp.take_along_axis(cdf_cols, jnp.clip(local_ids, 0, local_vocab - 1)[:,...]
    all_gather x2 -> x0, blocking collectives: 38.2 us -> none  [the longest x1 23.3 us: local_step(): shard_stats = lax.all_gather(jnp.stack([local_max, local_sum]), 'vp')]
    another operation x6 -> x0, local copies, waits for them, and re-layouts: 36.2 us -> none
    dot_general x1 -> x0, matrix products: 23.9 us -> none  [local_step(): logits = jnp.dot(hidden, w_local, preferred_element_type=jnp.float32)]
    add x2 -> x0, other arithmetic: 15.9 us -> none  [local_step(): cdf_cols = local_cdf + offset[:, None]]
    another operation x3 -> x0, other arithmetic: 11.8 us -> none
  transfers between devices with their start and end apart: 1 -> 0, of which waited for: 0 -> 0; matrix products, arithmetic and copies ran while one was open for 15% -> 0% of each run, Pallas kernels for 0% -> 0%
where the time goes in v2:
time: 198 us
  Pallas kernels  197 us (99%)
    pallas_call x1, Pallas kernels, local_step(): pl.pallas_call(functools.partial(exchange_kernel, size), out_shape=(pltpu...  194 us

profile of v2, /device:TPU:21, one launch (start us, length us, event | category | flops | bytes accessed | tf_op | source)
XLA Modules:
  0.0 198.0 jit_solution(4338359557318236918)
XLA Ops:
  0.6 193.6 %exchange.1 = (f32[16,64,2048]{2,1,0:T(8,128)S(1)}, f32[64,128]{1,0:T(8,128)S(1)}, f32[8,128]{1,0:T(8,128)S(1)}) custom-call(f32[8,128]{1,0:T(8,128)} %bitcast.3, s32[8,128]{1,0:T(8,128)} %bitcast.4, bf16[1024,4096]{1,0:T(8,128)(2,1)} %hid_ref.1, bf16[4096,2048]{1,0:T(8,128)(2,1)} %w_ref.1), custom_call_target="tpu_custom_call" | custom-call | tf_op jit(solution)/shard_map/exchange/pallas_call | solution.py:394
  194.2 3.5 %table.1 = (f32[64,32768]{1,0:T(8,128)}, f32[8,128]{1,0:T(8,128)}) custom-call(f32[16,64,2048]{2,1,0:T(8,128)S(1)} %get-tuple-element.7.recv_ref, f32[64,128]{1,0:T(8,128)S(1)} %get-tuple-element.8.so_ref, f32[8,128]{1,0:T(8,128)S(1)} %get-tuple-element.9.t_ref), custom_call_target="tpu_custom_call" | custom-call | tf_op jit(solution)/shard_map/table/pallas_call | solution.py:433

commit v3 on v2

--- a/solution.py
+++ b/solution.py
@@ -26,7 +26,7 @@
 def exchange_kernel(
     size, it_hbm, tgt_hbm, hid_ref, w_ref,
     recv_ref, so_ref, out_t_ref,
-    it_ref, tgt_ref, w_v, hid_v, tri_v, send_v, stat_mine, stat_recv, t_mine, t_recv,
+    it_ref, tgt_ref, w_v, hid_v, tri_v, state_v, send_v, stat_mine, stat_recv, t_mine, t_recv,
     row_sem, w_sem, h_sem, h0_sem, data_send, data_recv, stat_ssem, stat_rsem, pair_ssem, pair_rsem, t_ssem, t_rsem,
 ):
     me = lax.axis_index("vp")
@@ -51,7 +51,7 @@
 
     def w_copy(j, p):
         start, width = bounds[j]
-        here = (pl.ds(p * piece, piece), pl.ds(start, width))
+        here = (pl.ds(pl.multiple_of(p * piece, piece), piece), pl.ds(start, width))
         return pltpu.make_async_copy(w_ref.at[here], w_v.at[here], w_sem.at[j, p])
 
     def h_copy(p, side):
@@ -61,10 +61,12 @@
         )
 
     def h_first(q, side):
-        start = pl.multiple_of(chip_at(0, side) * rows, rows)
-        here = pl.ds(q * piece, piece)
+        chip = chip_at(0, 0) * (1 - side) + chip_at(0, 1) * side
+        start = pl.multiple_of(chip * rows, rows)
+        here = pl.ds(pl.multiple_of(q * piece, piece), piece)
+        there = pl.ds(pl.multiple_of(side * rows, rows), rows)
         return pltpu.make_async_copy(
-            hid_ref.at[pl.ds(start, rows), here], hid_v.at[0, pl.ds(side * rows, rows), here], h0_sem.at[q, side]
+            hid_ref.at[pl.ds(start, rows), here], hid_v.at[0, there, here], h0_sem.at[q, side]
         )
 
     row_copies = [
@@ -72,13 +74,17 @@
         pltpu.make_async_copy(tgt_hbm, tgt_ref, row_sem.at[1]),
     ]
     for q in range(parts):
-        for side in range(2):
-            h_first(q, side).start()
+        h_first(q, 0).start()
         w_copy(0, q).start()
+    for q in range(parts):
+        h_first(q, 1).start()
     for copy in row_copies:
         copy.start()
-    for k in range(1, size):
+    def greet(k, carry_):
         pl.semaphore_signal(barrier, inc=1, device_id={"vp": (me + k) % size}, device_id_type=MESH)
+        return carry_
+
+    lax.fori_loop(1, size, greet, 0)
     r_iota = lax.broadcasted_iota(jnp.int32, (block, block), 0)
     c_iota = lax.broadcasted_iota(jnp.int32, (block, block), 1)
     tri_v[...] = jnp.where(r_iota <= c_iota, 1.0, 0.0).astype(BF16)
@@ -98,20 +104,26 @@
         start, width = bounds[j]
         return jnp.dot(hid_v[p], w_v[:, start : start + width], preferred_element_type=F32)
 
-    def first_product():
-        width = bounds[0][1]
-        total = jnp.zeros((2 * rows, width), F32)
-        for q in range(parts):
-            for side in range(2):
-                h_first(q, side).wait()
-            w_copy(0, q).wait()
-            w_copy(1, q).start()
-            here = slice(q * piece, (q + 1) * piece)
-            total = total + jnp.dot(hid_v[0, :, here], w_v[here, :width], preferred_element_type=F32)
-        return total
-
-    def chunk(p, j, logits, temp, target, state):
-        top, carry, pick, stats = state
+    def first_product(side):
+        first_cols = pl.ds(0, bounds[0][1])
+        mine = pl.ds(pl.multiple_of(side * rows, rows), rows)
+
+        def add_piece(q, total):
+            h_first(q, side).wait()
+
+            @pl.when(side == 0)
+            def _():
+                w_copy(0, q).wait()
+                w_copy(1, q).start()
+
+            here = pl.ds(pl.multiple_of(q * piece, piece), piece)
+            return total + jnp.dot(hid_v[0, mine, here], w_v[here, first_cols], preferred_element_type=F32)
+
+        return lax.fori_loop(0, parts, add_piece, jnp.zeros((rows, bounds[0][1]), F32))
+
+    def chunk(p, j, logits, temp, target, state, at=0):
+        top, carry, pick = state
+        count = logits.shape[0]
         first_col, width = bounds[j]
         logits = logits * temp
         new_top = jnp.maximum(top, jnp.max(logits, axis=1, keepdims=True))
@@ -123,39 +135,43 @@
         rest = e - first.astype(F32)
         second = rest.astype(BF16)
         third = (rest - second.astype(F32)).astype(BF16)
-        col = lax.broadcasted_iota(jnp.int32, (2 * rows, block), 1).astype(F32)
+        col = lax.broadcasted_iota(jnp.int32, (count, block), 1).astype(F32)
         for t in range(width // block):
             cut = slice(t * block, (t + 1) * block)
             terms = jnp.concatenate([first[:, cut], second[:, cut], third[:, cut]], axis=0)
             sums = jnp.dot(terms, tri_v[...], preferred_element_type=F32)
-            run = (sums[: 2 * rows] + (sums[2 * rows : 4 * rows] + sums[4 * rows :])) + carry
+            run = (sums[:count] + (sums[count : 2 * count] + sums[2 * count :])) + carry
             base = first_col + t * block
-            send_v[p, :, base : base + block] = run
+            send_v[p, pl.ds(at, count), base : base + block] = run
             hit = (col + float(base)) == target
             pick = pick + jnp.sum(jnp.where(hit, run, 0.0), axis=1, keepdims=True)
             carry = run[:, block - 1 :]
-        stats = jnp.where(lane == j, new_top, stats)
-        return new_top, carry, pick, stats
-
-    def send(p, side, columns):
-        for core in range(2):
+        return new_top, carry, pick
+
+    def send(p, side, columns, chip=None):
+        chip = chip_at(p, side) if chip is None else chip
+        for k in range(2):
+            core = 1 - k
             pltpu.make_async_remote_copy(
-                src_ref=send_v.at[p, pl.ds(side * rows + core * half, half), columns],
+                src_ref=send_v.at[p, pl.ds(pl.multiple_of(side * rows + core * half, half), half), columns],
                 dst_ref=recv_ref.at[me, :, columns],
                 send_sem=data_send.at[p, side],
                 recv_sem=data_recv.at[me],
-                device_id={"vp": chip_at(p, side) * 2 + core},
+                device_id={"vp": chip * 2 + core},
                 device_id_type=MESH,
             ).start()
 
     whole = pl.ds(0, local_vocab)
 
-    def start_state():
-        column = jnp.zeros((2 * rows, 1), F32)
-        return column - jnp.inf, column, column, jnp.zeros((2 * rows, LANES), F32)
-
-    def finish(p, state):
-        _, carry, pick, stats = state
+    def start_state(count):
+        column = jnp.zeros((count, 1), F32)
+        return column - jnp.inf, column, column
+
+    def finish(p, tops, state):
+        _, carry, pick = state
+        stats = jnp.zeros((2 * rows, LANES), F32)
+        for j in range(CHUNKS):
+            stats = jnp.where(lane == j, tops[j], stats)
         stats = jnp.where(lane == CHUNKS, carry, stats)
         stats = jnp.where(lane == CHUNKS + 1, pick, stats)
         for side in range(2):
@@ -163,11 +179,27 @@
 
     for copy in row_copies:
         copy.wait()
-    temp0, target0 = row_params(0)
-    state = chunk(0, 0, first_product(), temp0, target0, start_state())
-    pl.semaphore_wait(barrier, size - 1)
-    for side in range(2):
-        send(0, side, pl.ds(*bounds[0]))
+
+    def first_side(side, carry_):
+        chip = chip_at(0, 0) * (1 - side) + chip_at(0, 1) * side
+        temp = to_column(it_ref[pl.ds(chip, 1)])
+        target = to_column((tgt_ref[pl.ds(chip, 1)] - me * local_vocab).astype(F32))
+        at = pl.multiple_of(side * rows, rows)
+        state = chunk(0, 0, first_product(side), temp, target, start_state(rows), at)
+        for k, column in enumerate(state + (temp, target)):
+            state_v[k, pl.ds(at, rows)] = column
+
+        @pl.when(side == 0)
+        def _():
+            pl.semaphore_wait(barrier, size - 1)
+
+        send(0, side, pl.ds(*bounds[0]), chip)
+        return carry_
+
+    lax.fori_loop(0, 2, first_side, 0)
+    state = tuple(state_v[k] for k in range(3))
+    temp0, target0 = state_v[3], state_v[4]
+    tops = [state[0]]
     for j in range(2, CHUNKS):
         for q in range(parts):
             w_copy(j, q).start()
@@ -178,18 +210,21 @@
         for q in range(parts):
             w_copy(j, q).wait()
         state = chunk(0, j, product(0, j), temp0, target0, state)
+        tops.append(state[0])
         for side in range(2):
             send(0, side, pl.ds(*bounds[j]))
-    finish(0, state)
+    finish(0, tops, state)
 
     def step(p, carry_):
         for side in range(2):
             h_copy(p, side).wait()
         temp, target = row_params(p)
-        state = start_state()
+        state = start_state(2 * rows)
+        tops = []
         for j in range(CHUNKS):
             state = chunk(p, j, product(p, j), temp, target, state)
-        finish(p, state)
+            tops.append(state[0])
+        finish(p, tops, state)
         return carry_
 
     lax.fori_loop(1, pairs, step, 0)
@@ -406,6 +441,7 @@
                 pltpu.VMEM((depth, local_vocab), BF16),
                 pltpu.VMEM((chips // 2, 2 * rows, depth), BF16),
                 pltpu.VMEM((block, block), BF16),
+                pltpu.VMEM((5, 2 * rows, 1), F32),
                 pltpu.VMEM((chips // 2, 2 * rows, local_vocab), F32),
                 pltpu.VMEM((2, chips // 2, 2, STATS, rows), F32),
                 pltpu.VMEM((2, 2, chips // 2, STATS, rows), F32),

time: 198 us -> 197 us (level); the launches traced: 198 us -> 194 us
  Pallas kernels: 197 us -> 194 us
    pallas_call x1, Pallas kernels: 194 us -> 190 us  [local_step(): pl.pallas_call(functools.partial(exchange_kernel, size), out_shape=(pltpu...]
where the time goes in v3:
time: 197 us; the launch traced here: 194 us
  Pallas kernels  194 us (98%)
    pallas_call x1, Pallas kernels, local_step(): pl.pallas_call(functools.partial(exchange_kernel, size), out_shape=(pltpu...  190 us

profile of v3, /device:TPU:21, one launch (start us, length us, event | category | flops | bytes accessed | tf_op | source)
XLA Modules:
  0.0 194.4 jit_solution(17995639600440981557)
XLA Ops:
  0.6 190.2 %exchange.1 = (f32[16,64,2048]{2,1,0:T(8,128)S(1)}, f32[64,128]{1,0:T(8,128)S(1)}, f32[8,128]{1,0:T(8,128)S(1)}) custom-call(f32[8,128]{1,0:T(8,128)} %bitcast.3, s32[8,128]{1,0:T(8,128)} %bitcast.4, bf16[1024,4096]{1,0:T(8,128)(2,1)} %hid_ref.1, bf16[4096,2048]{1,0:T(8,128)(2,1)} %w_ref.1), custom_call_target="tpu_custom_call" | custom-call | tf_op jit(solution)/shard_map/exchange/pallas_call | solution.py:429
  190.9 3.5 %table.1 = (f32[64,32768]{1,0:T(8,128)}, f32[8,128]{1,0:T(8,128)}) custom-call(f32[16,64,2048]{2,1,0:T(8,128)S(1)} %get-tuple-element.7.recv_ref, f32[64,128]{1,0:T(8,128)S(1)} %get-tuple-element.8.so_ref, f32[8,128]{1,0:T(8,128)S(1)} %get-tuple-element.9.t_ref), custom_call_target="tpu_custom_call" | custom-call | tf_op jit(solution)/shard_map/table/pallas_call | solution.py:469

commit v4 on v3

--- a/solution.py
+++ b/solution.py
@@ -10,16 +10,16 @@
 F32 = jnp.float32
 BF16 = jnp.bfloat16
 LANES = 128
-EIGHTHS = (1, 3, 4)
-CHUNKS = len(EIGHTHS)
+SIXTEENTHS = (1, 5, 10)
+CHUNKS = len(SIXTEENTHS)
 STATS = CHUNKS + 2
 
 
 def chunk_bounds(local_vocab):
     bounds, start = [], 0
-    for part in EIGHTHS:
-        bounds.append((start, part * local_vocab // 8))
-        start += part * local_vocab // 8
+    for part in SIXTEENTHS:
+        bounds.append((start, part * local_vocab // 16))
+        start += part * local_vocab // 16
     return bounds
 
 
@@ -27,7 +27,7 @@
     size, it_hbm, tgt_hbm, hid_ref, w_ref,
     recv_ref, so_ref, out_t_ref,
     it_ref, tgt_ref, w_v, hid_v, tri_v, state_v, send_v, stat_mine, stat_recv, t_mine, t_recv,
-    row_sem, w_sem, h_sem, h0_sem, data_send, data_recv, stat_ssem, stat_rsem, pair_ssem, pair_rsem, t_ssem, t_rsem,
+    row_sem, w_sem, h_sem, h0_sem, data_send, data_recv, here_sem, stat_ssem, stat_rsem, pair_ssem, pair_rsem, t_ssem, t_rsem,
 ):
     me = lax.axis_index("vp")
     chips = size // 2
@@ -80,11 +80,11 @@
         h_first(q, 1).start()
     for copy in row_copies:
         copy.start()
-    def greet(k, carry_):
-        pl.semaphore_signal(barrier, inc=1, device_id={"vp": (me + k) % size}, device_id_type=MESH)
-        return carry_
-
-    lax.fori_loop(1, size, greet, 0)
+    def ahead(steps, core):
+        return ((z + steps + chips) % chips) * 2 + core
+
+    for peer in [ahead(d, core) for d in (pairs - 1, 1 - pairs) for core in range(2)] + [z * 2 + (1 - c)]:
+        pl.semaphore_signal(barrier, inc=1, device_id={"vp": peer}, device_id_type=MESH)
     r_iota = lax.broadcasted_iota(jnp.int32, (block, block), 0)
     c_iota = lax.broadcasted_iota(jnp.int32, (block, block), 1)
     tri_v[...] = jnp.where(r_iota <= c_iota, 1.0, 0.0).astype(BF16)
@@ -191,12 +191,14 @@
 
         @pl.when(side == 0)
         def _():
-            pl.semaphore_wait(barrier, size - 1)
+            pl.semaphore_wait(barrier, 5)
 
         send(0, side, pl.ds(*bounds[0]), chip)
         return carry_
 
     lax.fori_loop(0, 2, first_side, 0)
+    for d in (pairs - 1, 1 - pairs):
+        pl.semaphore_signal(here_sem.at[0], inc=1, device_id={"vp": ahead(d, c)}, device_id_type=MESH)
     state = tuple(state_v[k] for k in range(3))
     temp0, target0 = state_v[3], state_v[4]
     tops = [state[0]]
@@ -214,6 +216,9 @@
         for side in range(2):
             send(0, side, pl.ds(*bounds[j]))
     finish(0, tops, state)
+    pl.semaphore_wait(here_sem.at[0], 2)
+    for d in (2, -2):
+        pl.semaphore_signal(here_sem.at[1], inc=1, device_id={"vp": ahead(d, c)}, device_id_type=MESH)
 
     def step(p, carry_):
         for side in range(2):
@@ -228,6 +233,7 @@
         return carry_
 
     lax.fori_loop(1, pairs, step, 0)
+    pl.semaphore_wait(here_sem.at[1], 2)
     two, one, ends = range(1, pairs)
     others = [(p, side) for p in range(pairs) for side in range(2) if (p, side) != (ends, 0)]
 
@@ -423,7 +429,7 @@
         local_vocab = w_local.shape[1]
         rows = batch // chips
         half = rows // 2
-        block = min(256, local_vocab // 8)
+        block = min(256, local_vocab // 16)
         vmem = pl.BlockSpec(memory_space=pltpu.VMEM)
         hbm = pl.BlockSpec(memory_space=pl.ANY)
         recv, so, t_all = pl.pallas_call(
@@ -453,6 +459,7 @@
                 pltpu.SemaphoreType.DMA((4, 2)),
                 pltpu.SemaphoreType.DMA((chips // 2, 2)),
                 pltpu.SemaphoreType.DMA((size,)),
+                pltpu.SemaphoreType.REGULAR((2,)),
                 pltpu.SemaphoreType.DMA((chips // 2,)),
                 pltpu.SemaphoreType.DMA((chips // 2,)),
                 pltpu.SemaphoreType.DMA((3,)),

time: 197 us -> 198 us (level)
  no operation moved by 1% of the time
where the time goes in v4:
time: 198 us; the launch traced here: 195 us
  Pallas kernels  194 us (98%)
    pallas_call x1, Pallas kernels, local_step(): pl.pallas_call(functools.partial(exchange_kernel, size), out_shape=(pltpu...  191 us

profile of v4, /device:TPU:21, one launch (start us, length us, event | category | flops | bytes accessed | tf_op | source)
XLA Modules:
  0.0 195.2 jit_solution(6232130749366501779)
XLA Ops:
  0.6 190.9 %exchange.1 = (f32[16,64,2048]{2,1,0:T(8,128)S(1)}, f32[64,128]{1,0:T(8,128)S(1)}, f32[8,128]{1,0:T(8,128)S(1)}) custom-call(f32[8,128]{1,0:T(8,128)} %bitcast.3, s32[8,128]{1,0:T(8,128)} %bitcast.4, bf16[1024,4096]{1,0:T(8,128)(2,1)} %hid_ref.1, bf16[4096,2048]{1,0:T(8,128)(2,1)} %w_ref.1), custom_call_target="tpu_custom_call" | custom-call | tf_op jit(solution)/shard_map/exchange/pallas_call | solution.py:435
  191.5 3.6 %table.1 = (f32[64,32768]{1,0:T(8,128)}, f32[8,128]{1,0:T(8,128)}) custom-call(f32[16,64,2048]{2,1,0:T(8,128)S(1)} %get-tuple-element.7.recv_ref, f32[64,128]{1,0:T(8,128)S(1)} %get-tuple-element.8.so_ref, f32[8,128]{1,0:T(8,128)S(1)} %get-tuple-element.9.t_ref), custom_call_target="tpu_custom_call" | custom-call | tf_op jit(solution)/shard_map/table/pallas_call | solution.py:476
